TPU v7x, 32 devices: a whole 2x2x4 slice. The times are simulated.
32 devices in a mesh: grp: 2 (over y), row: 4 (over x, core), col: 4 (over z).
Axes of the slice: x: 2, y: 2, z: 4, core: 2. Of those that a mesh axis runs over, the one named last changes fastest.
Arguments:
- perturbation: bfloat16 [4, 12000, 12000], P('grp', 'row', 'col'), parts along dimension 0, may hold values from -96 to 96
- occ_coeffs: bfloat16 [12000, 2000], P('row', 'col'), may hold values from -0.0546875 to 0.0546875
- vir_coeffs: bfloat16 [12000, 512], P('col', 'row'), may hold values from -0.0546875 to 0.0546875
- occ_energies: float32 [2000], replicated, may hold values from -1 to -0.1
- vir_energies: float32 [512], replicated, may hold values from 0.1 to 1.5
Outputs:
- density_response: bfloat16 [4, 12000, 12000], P('grp', 'row', 'col'), parts along dimension 0
There are 2 independent parts, one for each index of `grp`. A program takes and returns all parts, laid end to end along the dimension named above; an argument that names none is the same for every part. Nothing has to cross between parts.
All inputs are finite; a program needn't handle non-finite values.
Results may differ from a plain program's by a relative error of at most 0.0098.
Values may be sent and summed in bfloat16 or wider, within the bound.
A program may use at most 192 MiB of HBM per device.

v0:
```python
import jax
import jax.numpy as jnp
from jax import lax
from jax.sharding import PartitionSpec as P

BF16 = jnp.bfloat16
F32 = jnp.float32


def per_device(perturbation, occ_coeffs, vir_coeffs, occ_energies, vir_energies):
    vir_rows = lax.all_gather(vir_coeffs, "row", axis=1, tiled=True)
    occ_parts = lax.all_gather(occ_coeffs, "col")
    cols, _, width = occ_parts.shape
    image = jnp.einsum(
        "pij,jv->piv", perturbation, vir_rows, preferred_element_type=F32
    ).astype(BF16)
    part = jnp.einsum("cio,piv->pcov", occ_parts, image, preferred_element_type=F32).astype(BF16)
    coupling = lax.psum(part, ("row", "col"))
    gaps = occ_energies.reshape(cols, width)[:, :, None] - vir_energies[None, None, :]
    response = (coupling.astype(F32) / gaps[None]).astype(BF16)
    mixed = jnp.einsum("cio,pcov->piv", occ_parts, response, preferred_element_type=F32).astype(BF16)
    return jnp.einsum("piv,jv->pij", mixed, vir_rows, preferred_element_type=F32).astype(BF16)


def solution(mesh):
    placed = (P("grp", "row", "col"), P("row", "col"), P("col", "row"), P(), P())
    return jax.shard_map(
        per_device, mesh=mesh, in_specs=placed, out_specs=P("grp", "row", "col"), check_vma=False
    )
```

profile of v0, /device:TPU:0, one launch (start us, length us, event | category | flops | bytes accessed | tf_op | source)
XLA Modules:
  0.0 448.0 jit_solution(10581064769501468559)
XLA Ops:
  6.5 0.0 all-gather.4.cloned.1.call-start
  6.5 0.7 all-gather.4.cloned.1.call-update
  7.3 0.0 all-gather.6.cloned.1.call-start
  7.3 0.7 all-gather.6.cloned.1.call-update
  8.0 0.0 all-reduce.2.cloned.1.call-start
  8.1 32.1 %all-gather.4.cloned.1.call-done = bf16[3000,512]{1,0:T(8,128)(2,1)} async-done(((bf16[3000,128]{1,0:T(8,128)(2,1)}), bf16[3000,512]{1,0:T(8,128)(2,1)}) %all-gather.4.cloned.1.call-update) | async-done | bytes 3072016 | tf_op jit(solution)/shard_map/all_gather | solution.py:11
  40.1 25.8 %fusion.45 = bf16[2,3000,512,1]{2,1,3,0:T(8,128)(2,1)} fusion(bf16[2,3000,3000]{2,1,0:T(8,128)(2,1)} %param.5, bf16[3000,512]{1,0:T(8,128)(2,1)} %all-gather.4.cloned.1.call-done), kind=kOutput, calls=%fused_computation.5.clone.clone.clone.1 | convolution fusion | flops 18435072000 | bytes 45216000 | tf_op jit(solution)/shard_map/pij,jv->piv/dot_general | solution.py:14
  66.0 189.1 %all-gather.6.cloned.1.call-done = bf16[12000,500]{1,0:T(8,128)(2,1)} async-done(((bf16[3000,500]{1,0:T(8,128)(2,1)}), bf16[12000,500]{1,0:T(8,128)(2,1)}) %all-gather.6.cloned.1.call-update) | async-done | bytes 12000016 | tf_op jit(solution)/shard_map/all_gather | solution.py:12
  255.1 19.1 %fusion.17 = bf16[2,512,4,500]{1,3,2,0:T(8,128)(2,1)} fusion(bf16[4,3000,500,1]{2,1,0,3:T(8,128)(2,1)} %bitcast.58, bf16[2,3000,512,1]{2,1,3,0:T(8,128)(2,1)} %fusion.45), kind=kOutput, calls=%fused_computation.12 | convolution fusion | flops 12290048000 | bytes 22240000 | tf_op jit(solution)/shard_map/cio,piv->pcov/dot_general | solution.py:17
  274.2 0.0 copy-start
  274.2 0.0 copy-start.1
  274.2 7.8 %copy.10 = bf16[2,512,4,500]{3,2,1,0:T(4,128)(2,1)} copy(bf16[2,512,4,500]{1,3,2,0:T(8,128)(2,1)} %fusion.17) | data formatting | bytes 8192000
  282.0 0.0 all-reduce.2.cloned.1.call-update
  282.0 0.0 copy-done
  282.1 0.1 sub.19
  282.1 0.0 copy-done.1
  282.1 2.8 broadcast_subtract_fusion
  285.0 106.6 %all-reduce.2.cloned.1.call-done = bf16[2,4,500,512]{2,1,3,0:T(4,128)(2,1)} async-done(((bf16[2,4,500,512]{2,1,3,0:T(4,128)(2,1)}), bf16[2,4,500,512]{2,1,3,0:T(4,128)(2,1)}) %all-reduce.2.cloned.1.call-update) | async-done | bytes 4096016 | tf_op jit(solution)/shard_map/psum | solution.py:18
  391.5 5.5 %fusion = bf16[2,4,500,512]{2,1,3,0:T(4,128)(2,1)S(1)} fusion(bf16[2,4,500,512]{2,1,3,0:T(4,128)(2,1)} %all-reduce.2.cloned.1.call-done, f32[4,500,512]{1,0,2:T(4,128)} %broadcast_subtract_fusion), kind=kLoop, calls=%fused_computation.3 | loop fusion | flops 6144000 | bytes 12288000 | tf_op jit(solution)/shard_map/convert_element_type | solution.py:20
  397.1 16.8 %fusion.41 = bf16[2,3000,512]{2,1,0:T(8,128)(2,1)} fusion(bf16[4,3000,500,1]{2,1,0,3:T(8,128)(2,1)} %bitcast.59, bf16[2,4,500,512]{2,1,3,0:T(4,128)(2,1)S(1)} %fusion), kind=kOutput, calls=%fused_computation.6.clone.1 | convolution fusion | flops 12291072000 | bytes 22240000 | tf_op jit(solution)/shard_map/cio,pcov->piv/dot_general | solution.py:21
  413.9 27.6 %convolution_convert_fusion = bf16[2,3000,3000]{2,1,0:T(8,128)(2,1)} fusion(bf16[3000,512]{1,0:T(8,128)(2,1)} %all-gather.4.cloned.1.call-done, bf16[2,3000,512]{2,1,0:T(8,128)(2,1)} %fusion.41), kind=kOutput, calls=%fused_computation | convolution fusion | flops 18449999872 | bytes 45216000 | tf_op jit(solution)/shard_map/piv,jv->pij/dot_general | solution.py:22
Async XLA Ops:
  6.5 33.6 %all-gather.4.cloned.1.call-start = ((), (), s32[]{:S(2)}) async-start(), calls=%async_computation | async-start | bytes 3840000 | tf_op jit(solution)/shard_map/all_gather | solution.py:11
  7.3 247.8 %all-gather.6.cloned.1.call-start = ((), (), s32[]{:S(2)}) async-start(), calls=%async_computation.2 | async-start | bytes 15360000 | tf_op jit(solution)/shard_map/all_gather | solution.py:12
  8.0 383.5 %all-reduce.2.cloned.1.call-start = ((), (), s32[]{:S(2)}) async-start(), calls=%async_computation.1 | async-start | bytes 8388608 | tf_op jit(solution)/shard_map/psum | solution.py:18
  274.2 7.9 %copy-start = (f32[2000]{0:T(1024)S(1)}, f32[2000]{0:T(1024)}, u32[]{:S(2)}) copy-start(f32[2000]{0:T(1024)} %param.8) | copy-start | bytes 24004
  274.2 8.0 %copy-start.1 = (f32[512]{0:T(512)S(1)}, f32[512]{0:T(512)}, u32[]{:S(2)}) copy-start(f32[512]{0:T(512)} %param.9) | copy-start | bytes 6148
Sparse Core Ops, SparseCore 0:
  8.9 31.1 all-gather.3
  41.7 213.3 all-gather.5
  282.2 109.3 all-reduce.1
where the time goes:
time: 448 us
  waiting for transfers between devices  329 us (73%)
  matrix products  89.4 us (20%)
  between operations  13.1 us (3%)
  other arithmetic  8.38 us (2%)
  local copies, waits for them, and re-layouts  7.93 us (2%)
    all_gather x1, waiting for transfers between devices, per_device(): occ_parts = lax.all_gather(occ_coeffs, 'col')  189 us
    psum x1, waiting for transfers between devices, per_device(): coupling = lax.psum(part, ('row', 'col'))  107 us
    all_gather x1, waiting for transfers between devices, per_device(): vir_rows = lax.all_gather(vir_coeffs, 'row', axis=1, tiled=True)  32.1 us
    dot_general x1, matrix products, per_device(): jnp.einsum('piv,jv->pij', mixed, vir_rows, preferred_element_type=F32)  27.6 us
    dot_general x1, matrix products, per_device(): jnp.einsum('pij,jv->piv', perturbation, vir_rows, preferred_element_type=...  25.8 us
    dot_general x1, matrix products, per_device(): jnp.einsum('cio,piv->pcov', occ_parts, image, preferred_element_type=F32)  19.1 us
    dot_general x1, matrix products, per_device(): jnp.einsum('cio,pcov->piv', occ_parts, response, preferred_element_type=F32)  16.8 us
  transfers between devices with their start and end apart: 3, of which 3 were waited for; matrix products, arithmetic and copies ran while one was open for 6% of the time, Pallas kernels for 0%

commit v1 on v0

v1 whole, which is shorter than its diff:
```python
import functools

import jax
import jax.numpy as jnp
from jax import lax
from jax.experimental import pallas as pl
from jax.experimental.pallas import tpu as pltpu
from jax.sharding import PartitionSpec as P

BF16 = jnp.bfloat16
F32 = jnp.float32
MESH = pl.DeviceIdType.MESH
NT = (((1,), (1,)), ((), ()))
NN = (((1,), (0,)), ((), ()))
PIECES = 4


def up(value, step):
    return -(-value // step) * step


def flip(index, bit):
    return index + bit - 2 * bit * ((index // bit) % 2)


def pick(position, options):
    value = jnp.int32(0)
    for index, option in enumerate(options):
        value = value + jnp.where(position == index, jnp.int32(option), jnp.int32(0))
    return value


def arrivals(cols, position):
    order = [(position, 0), (position, 1)]
    for slot in range(cols - 1):
        blocks = [b for b in (position - 1 - slot, position + 1 + slot) if 0 <= b < cols]
        order += [(b, 0) for b in blocks] + [(b, 1) for b in blocks]
    return order


def gather_kernel(
    dims,
    h_hbm, occ_hbm, vir_hbm, occ_e, vir_e,
    mixed_hbm, virt_hbm,
    occ, virt, hbuf, image, part, rs1, rs2s, rs2r, resp, acc, stage,
    loc_sem, h_sem, vs_sem, vr_sem, zs_sem, zr_sem, ys_sem, yr_sem,
    a_s, a_r, b_s, b_r, c_s, c_r, d_s, d_r, o_sem,
):
    rows, cols = dims["rows"], dims["cols"]
    pert, ni, hb, nb = dims["pert"], dims["ni"], dims["hb"], dims["nb"]
    nv, ip, piece, wh = dims["nv"], dims["ip"], dims["piece"], dims["wh"]
    pv = pert * nv
    pr = pv // rows
    ps = pr // cols
    grp, row, col = lax.axis_index("grp"), lax.axis_index("row"), lax.axis_index("col")
    other = 1 - grp

    barrier = pltpu.get_barrier_semaphore()
    for d in range(1, rows):
        pl.semaphore_signal(barrier, inc=1, device_id={"row": (row + d) % rows}, device_id_type=MESH)
    for e in range(1, cols):
        pl.semaphore_signal(barrier, inc=1, device_id={"col": (col + e) % cols}, device_id_type=MESH)
    pl.semaphore_signal(barrier, inc=1, device_id={"grp": other}, device_id_type=MESH)

    def half_copy(half, sem):
        return pltpu.make_async_copy(
            occ_hbm.at[:, pl.ds(pl.multiple_of(half * wh, wh), wh)], occ.at[col, half], loc_sem.at[sem]
        )

    half_copy(grp, 0).start()
    vir_copy = pltpu.make_async_copy(vir_hbm, virt.at[row], loc_sem.at[2])
    vir_copy.start()
    half_copy(other, 1).start()

    def h_copy(n, act):
        p, b, slot = n // nb, n % nb, n % 2
        last = ni - (nb - 1) * hb

        def go(size):
            copy = pltpu.make_async_copy(
                h_hbm.at[p, pl.ds(pl.multiple_of(b * hb, hb), size)], hbuf.at[slot, pl.ds(0, size)], h_sem.at[slot]
            )
            act(copy)

        if nb == 1:
            act(pltpu.make_async_copy(h_hbm.at[p], hbuf.at[slot], h_sem.at[slot]))
        elif last == hb:
            go(hb)
        else:
            pl.when(b < nb - 1)(lambda: go(hb))
            pl.when(b == nb - 1)(lambda: go(last))

    h_copy(jnp.int32(0), lambda c: c.start())
    pl.semaphore_wait(barrier, rows + cols - 1)

    def vir_send(block, target, n):
        return pltpu.make_async_remote_copy(
            src_ref=virt.at[block], dst_ref=virt.at[block], send_sem=vs_sem.at[n], recv_sem=vr_sem.at[block],
            device_id={"row": target}, device_id_type=MESH,
        )

    vir_copy.wait()
    top = rows // 2
    vir_send(row, flip(row, top), 0).start()

    def z_send(block, q, target, way):
        ref = occ.at[block, grp, pl.ds(q * piece, piece)]
        return pltpu.make_async_remote_copy(
            src_ref=ref, dst_ref=ref, send_sem=zs_sem.at[way, block], recv_sem=zr_sem.at[block, q],
            device_id={"col": target}, device_id_type=MESH,
        )

    def y_send(block, q):
        ref = occ.at[block, grp, pl.ds(q * piece, piece)]
        return pltpu.make_async_remote_copy(
            src_ref=ref, dst_ref=ref, send_sem=ys_sem.at[block], recv_sem=yr_sem.at[block],
            device_id={"grp": other}, device_id_type=MESH,
        )

    half_copy(grp, 0).wait()
    for q in range(PIECES):
        pl.when(col >= 1)(lambda q=q: z_send(col, q, col - 1, 0).start())
        pl.when(col <= cols - 2)(lambda q=q: z_send(col, q, col + 1, 1).start())

    def pump(slot, q):
        def from_left():
            block = col - 1 - slot
            z_send(block, q, 0, 1).wait_recv()
            pl.when(col <= cols - 2)(lambda: z_send(block, q, col + 1, 1).start())
            y_send(block, q).start()

        def from_right():
            block = col + 1 + slot
            z_send(block, q, 0, 0).wait_recv()
            pl.when(col >= 1)(lambda: z_send(block, q, col - 1, 0).start())
            y_send(block, q).start()

        pl.when(col - 1 - slot >= 0)(from_left)
        pl.when(col + 1 + slot <= cols - 1)(from_right)

    pump(0, 0)
    held, bit = [0], top
    while bit >= 1:
        if bit != top:
            for h_at, h in enumerate(held):
                vir_send(flip_all(row, h), flip(row, bit), len(held) - 1 + h_at).start()
        for h in held:
            vir_send(flip_all(row, h + bit), row, 0).wait_recv()
        held = held + [h + bit for h in held]
        bit //= 2
    virt_out = pltpu.make_async_copy(virt, virt_hbm, loc_sem.at[2])
    virt_out.start()
    if PIECES > 1:
        pump(0, 1)

    steps = pert * nb

    def image_step(n, carry):
        pl.when(n + 1 < steps)(lambda: h_copy(n + 1, lambda c: c.start()))
        h_copy(n, lambda c: c.wait())
        p, b, slot = n // nb, n % nb, n % 2
        lhs = virt[...].reshape(nv, virt.shape[2])
        value = lax.dot_general(lhs, hbuf[slot], NT, preferred_element_type=F32)
        basis = lax.broadcasted_iota(jnp.int32, (1, hb), 1) + b * hb
        value = jnp.where(basis < ni, value, 0.0).astype(BF16)
        at = pl.ds(pl.multiple_of(p * nv, nv), nv)
        if nb == 1:
            image[at, :] = jnp.zeros((nv, ip), BF16)
            image[at, 0:hb] = value
        else:
            image[at, pl.ds(pl.multiple_of(b * hb, hb), hb)] = value
        for q in range(2, PIECES):
            at = min(steps - 1, (q - 1) * steps // (PIECES - 1))
            pl.when(n == at)(lambda q=q: pump(0, q))
        return carry

    lax.fori_loop(0, steps, image_step, 0)
    half_copy(other, 1).wait()

    order = [arrivals(cols, position) for position in range(cols)]

    def chunk(s):
        block = pick(col, [order[position][s][0] for position in range(cols)])
        second = pick(col, [order[position][s][1] for position in range(cols)])
        half = grp * (1 - second) + other * second
        return block, second, half

    def rs1_send(block, half, d, target):
        return pltpu.make_async_remote_copy(
            src_ref=part.at[block, half, target], dst_ref=rs1.at[block, half, d - 1],
            send_sem=a_s.at[block, half], recv_sem=a_r.at[block, half],
            device_id={"row": target}, device_id_type=MESH,
        )

    def make_part(s):
        block, second, half = chunk(s)
        if s >= 2:
            def await_second():
                pltpu.make_async_copy(occ.at[block, half], occ.at[block, half], yr_sem.at[block]).wait()
            pl.when(second == 1)(await_second)

        def body(d, carry):
            target = (row + d) % rows
            lhs = image[pl.ds(pl.multiple_of(target * pr, pr), pr), :]
            value = lax.dot_general(lhs, occ[block, half], NN, preferred_element_type=F32)
            part[block, half, target] = value.astype(BF16)
            pl.when(d < rows)(lambda: rs1_send(block, half, d, target).start())
            return carry

        lax.fori_loop(1, rows + 1, body, 0)

    def rs2_send(block, half, e):
        target = (col + e) % cols
        return pltpu.make_async_remote_copy(
            src_ref=rs2s.at[block, half, target], dst_ref=rs2r.at[block, half, e - 1],
            send_sem=b_s.at[block, half], recv_sem=b_r.at[block, half],
            device_id={"col": target}, device_id_type=MESH,
        )

    def combine(s):
        block, second, half = chunk(s)
        pltpu.make_async_copy(rs1.at[block, half], rs1.at[block, half], a_r.at[block, half]).wait()
        total = part[block, half, row].astype(F32)
        for d in range(rows - 1):
            total = total + rs1[block, half, d].astype(F32)
        rs2s[block, half] = total.reshape(cols, ps, wh).astype(BF16)
        for e in range(1, cols):
            rs2_send(block, half, e).start()

    def pair(d, second):
        half = grp if second == 0 else other
        return [(cols // 2 - 1 - d, half), (cols // 2 + d, half)]

    def ag1_send(block, half, e):
        ref = resp.at[block, half, row, col]
        return pltpu.make_async_remote_copy(
            src_ref=ref, dst_ref=ref, send_sem=c_s.at[block, half], recv_sem=c_r.at[block, half],
            device_id={"col": (col + e) % cols}, device_id_type=MESH,
        )

    def ag2_send(block, half, d):
        ref = resp.at[block, half, row]
        return pltpu.make_async_remote_copy(
            src_ref=ref, dst_ref=ref, send_sem=d_s.at[block, half], recv_sem=d_r.at[block, half],
            device_id={"row": (row + d) % rows}, device_id_type=MESH,
        )

    def respond(d, second):
        for block, half in pair(d, second):
            pltpu.make_async_copy(rs2r.at[block, half], rs2r.at[block, half], b_r.at[block, half]).wait()
            total = rs2s[block, half, col].astype(F32)
            for e in range(cols - 1):
                total = total + rs2r[block, half, e].astype(F32)
            gaps = occ_e[block, half] - vir_e[pl.ds(pl.multiple_of(row * pr + col * ps, ps), ps), :]
            resp[block, half, row, col] = (total / gaps).astype(BF16)
            for e in range(1, cols):
                ag1_send(block, half, e).start()

    def spread(d, second):
        for block, half in pair(d, second):
            some = resp.at[block, half, row, pl.ds(0, cols - 1)]
            pltpu.make_async_copy(some, some, c_r.at[block, half]).wait()
            for e in range(1, rows):
                ag2_send(block, half, e).start()

    tile = dims["tile"]
    tiles = ip // tile

    def out_copy(n, slot):
        return [
            pltpu.make_async_copy(
                stage.at[slot, p], mixed_hbm.at[p, pl.ds(pl.multiple_of(n * tile, tile), tile)], o_sem.at[slot]
            )
            for p in range(pert)
        ]

    def mix(d, second, first, last):
        chunks = pair(d, second)
        for block, half in chunks:
            some = resp.at[block, half, pl.ds(0, rows - 1)]
            pltpu.make_async_copy(some, some, d_r.at[block, half]).wait()

        def body(n, carry):
            at = pl.ds(pl.multiple_of(n * tile, tile), tile)
            if last:
                def free():
                    for copy in out_copy(n - 2, n % 2):
                        copy.wait()
                pl.when(n >= 2)(free)
            for p in range(pert):
                across = rows // pert
                total = None
                for block, half in chunks:
                    rhs = resp[block, half, pl.ds(p * across, across)]
                    rhs = rhs.astype(F32).reshape(nv, wh).astype(BF16)
                    value = lax.dot_general(occ[block, half, at], rhs, NT, preferred_element_type=F32)
                    total = value if total is None else total + value
                if not first:
                    total = total + acc[p, at]
                if last:
                    stage[n % 2, p] = total.astype(BF16)
                else:
                    acc[p, at] = total
            if last:
                for copy in out_copy(n, n % 2):
                    copy.start()
            return carry

        lax.fori_loop(0, tiles, body, 0)
        if last:
            for n in range(max(0, tiles - 2), tiles):
                for copy in out_copy(n, n % 2):
                    copy.wait()

    left = [(t, q) for t in range(1, cols - 1) for q in range(PIECES)]

    def through(slot):
        while left and left[0][0] <= slot:
            pump(*left.pop(0))

    def some_pumps(count, slot):
        for _ in range(count):
            if left and left[0][0] <= slot:
                pump(*left.pop(0))

    make_part(0)
    make_part(1)
    combine(0)
    make_part(2)
    combine(1)
    some_pumps(2, 1)
    make_part(3)
    combine(2)
    some_pumps(1, 1)
    combine(3)
    through(1)
    started = False
    for s in range(4, cols + 1):
        through((s - 2) // 2)
        make_part(s)
        some_pumps(1, (s - 2) // 2 + 1)
        combine(s)
    for d in range(cols // 2):
        s = cols + 2 * d
        if d > 0:
            through((s - 2) // 2)
            make_part(s)
            combine(s)
        final = d == cols // 2 - 1
        make_part(s + 1)
        respond(d, 0)
        some_pumps(1, s // 2)
        combine(s + 1)
        spread(d, 0)
        some_pumps(1, s // 2)
        respond(d, 1)
        mix(d, 0, not started, False)
        started = True
        some_pumps(1, s // 2)
        spread(d, 1)
        mix(d, 1, False, final)

    virt_out.wait()
    for n in range(rows - 1):
        vir_send(row, row, n).wait_send()
    for block in range(cols):
        whole = occ.at[block, 0]

        def sent(sem, whole=whole):
            pltpu.make_async_copy(whole, whole, sem).wait()

        pl.when((col >= 1) & (col <= block))(lambda: sent(zs_sem.at[0, block]))
        pl.when((col <= cols - 2) & (col >= block))(lambda: sent(zs_sem.at[1, block]))
        pl.when(col != block)(lambda: sent(ys_sem.at[block]))
        for half in range(2):
            sizes = (
                (a_s, rs1.at[block, half]),
                (b_s, rs2r.at[block, half]),
                (c_s, resp.at[block, half, 0, pl.ds(0, cols - 1)]),
                (d_s, resp.at[block, half, pl.ds(0, rows - 1)]),
            )
            for sem, ref in sizes:
                pltpu.make_async_copy(ref, ref, sem.at[block, half]).wait()


def flip_all(index, mask):
    bit = 1
    while bit <= mask:
        if mask & bit:
            index = flip(index, bit)
        bit *= 2
    return index


def final_kernel(mixed_ref, virt_ref, out_ref):
    out_ref[0] = lax.dot_general(mixed_ref[0], virt_ref[...], NN, preferred_element_type=F32).astype(BF16)


def per_device(mesh, perturbation, occ_coeffs, vir_coeffs, occ_energies, vir_energies):
    rows, cols = mesh.shape["row"], mesh.shape["col"]
    pert, ni, nj = perturbation.shape
    width = occ_coeffs.shape[1]
    nv = vir_coeffs.shape[1] * rows
    wh = up(-(-width // 2), 128)
    piece = up(-(-ni // PIECES), 64)
    ip = piece * PIECES
    hb = 512 if ni % 8 == 0 and ni > 512 else ni
    nb = -(-ni // hb)
    ip = up(max(nb * hb, ip), 256)
    piece = ip // PIECES
    pv = pert * nv
    pr = pv // rows
    ps = pr // cols
    tile = 512 if ip % 512 == 0 else 256
    dims = dict(rows=rows, cols=cols, pert=pert, ni=ni, hb=hb, nb=nb, nv=nv, ip=ip, piece=piece, wh=wh, tile=tile)

    occ_padded = jnp.pad(occ_coeffs, ((0, ip - ni), (0, 2 * wh - width)))
    vir_t = vir_coeffs.T
    occ_e = jnp.pad(occ_energies.reshape(cols, width), ((0, 0), (0, 2 * wh - width)), constant_values=-1.0)
    occ_e = occ_e.reshape(cols, 2, 1, wh)
    vir_e = jnp.tile(vir_energies, pert)[:, None]

    any_space = pl.BlockSpec(memory_space=pl.ANY)
    vmem = pl.BlockSpec(memory_space=pltpu.VMEM)
    dma = pltpu.SemaphoreType.DMA
    mixed, virt = pl.pallas_call(
        functools.partial(gather_kernel, dims),
        out_shape=(
            jax.ShapeDtypeStruct((pert, ip, nv), BF16),
            jax.ShapeDtypeStruct((rows, nv // rows, nj), BF16),
        ),
        in_specs=[any_space, any_space, any_space, vmem, vmem],
        out_specs=(any_space, any_space),
        scratch_shapes=[
            pltpu.VMEM((cols, 2, ip, wh), BF16),
            pltpu.VMEM((rows, nv // rows, nj), BF16),
            pltpu.VMEM((2, hb, nj), BF16),
            pltpu.VMEM((pv, ip), BF16),
            pltpu.VMEM((cols, 2, rows, pr, wh), BF16),
            pltpu.VMEM((cols, 2, rows - 1, pr, wh), BF16),
            pltpu.VMEM((cols, 2, cols, ps, wh), BF16),
            pltpu.VMEM((cols, 2, cols - 1, ps, wh), BF16),
            pltpu.VMEM((cols, 2, rows, cols, ps, wh), BF16),
            pltpu.VMEM((pert, ip, nv), F32),
            pltpu.VMEM((2, pert, tile, nv), BF16),
            dma((3,)), dma((2,)), dma((rows,)), dma((rows,)),
            dma((2, cols)), dma((cols, PIECES)), dma((cols,)), dma((cols,)),
            dma((cols, 2)), dma((cols, 2)), dma((cols, 2)), dma((cols, 2)),
            dma((cols, 2)), dma((cols, 2)), dma((cols, 2)), dma((cols, 2)),
            dma((2,)),
        ],
        compiler_params=pltpu.CompilerParams(
            collective_id=0, has_side_effects=True, vmem_limit_bytes=67043328
        ),
        name="gather",
    )(perturbation, occ_padded, vir_t, occ_e, vir_e)

    virt = virt.reshape(nv, nj)
    block = 384 if ip % 384 == 0 else 256
    return pl.pallas_call(
        final_kernel,
        out_shape=jax.ShapeDtypeStruct((pert, ni, nj), BF16),
        grid=(pert, ip // block),
        in_specs=[
            pl.BlockSpec((1, block, nv), lambda p, i: (p, i, 0)),
            pl.BlockSpec((nv, nj), lambda p, i: (0, 0)),
        ],
        out_specs=pl.BlockSpec((1, block, nj), lambda p, i: (p, i, 0)),
        compiler_params=pltpu.CompilerParams(vmem_limit_bytes=56 * 1024 * 1024),
        name="final",
    )(mixed, virt)


def solution(mesh):
    placed = (P("grp", "row", "col"), P("row", "col"), P("col", "row"), P(), P())
    return jax.shard_map(
        functools.partial(per_device, mesh), mesh=mesh, in_specs=placed,
        out_specs=P("grp", "row", "col"), check_vma=False,
    )
```

time: 448 us -> 246 us (0.55)
  waiting for transfers between devices: 329 us -> 0 us
  Pallas kernels: 0 us -> 235 us
  matrix products: 89.4 us -> 0 us
  between operations: 13.1 us -> 0.01 us
  other arithmetic: 8.38 us -> 0 us
    pallas_call x0 -> x2, Pallas kernels: none -> 235 us  [the longest x1 209 us: per_device(): pl.pallas_call(functools.partial(gather_kernel, dims), out_shape=(jax.Sha...]
    all_gather x2 -> x0, waiting for transfers between devices: 221 us -> none  [the longest x1 189 us: per_device(): occ_parts = lax.all_gather(occ_coeffs, 'col')]
    psum x1 -> x0, waiting for transfers between devices: 107 us -> none  [per_device(): coupling = lax.psum(part, ('row', 'col'))]
    dot_general x4 -> x0, matrix products: 89.4 us -> none  [the longest x1 27.6 us: per_device(): jnp.einsum('piv,jv->pij', mixed, vir_rows, preferred_element_type=F32)]
    convert_element_type x1 -> x0, other arithmetic: 5.54 us -> none  [per_device(): response = (coupling.astype(F32) / gaps[None]).astype(BF16)]
  transfers between devices with their start and end apart: 3 -> 0, of which waited for: 3 -> 0; matrix products, arithmetic and copies ran while one was open for 6% -> 0% of each run, Pallas kernels for 0% -> 0%
where the time goes in v1:
time: 246 us; the launch traced here: 244 us
  Pallas kernels  235 us (96%)
  local copies, waits for them, and re-layouts  9.41 us (4%)
    pallas_call x1, Pallas kernels, per_device(): pl.pallas_call(functools.partial(gather_kernel, dims), out_shape=(jax.Sha...  209 us
    pallas_call x1, Pallas kernels, per_device(): pl.pallas_call(final_kernel, out_shape=jax.ShapeDtypeStruct((pert, ni, nj...  26 us

profile of v1, /device:TPU:0, one launch (start us, length us, event | category | flops | bytes accessed | tf_op | source)
XLA Modules:
  0.0 244.3 jit_solution(11002393495202691758)
XLA Ops:
  0.0 0.7 broadcast_bitcast_fusion
  0.7 0.8 reshape.10
  1.5 0.6 reshape.11.occ_e
  2.1 1.1 copy.10
  3.2 2.3 copy.7
  5.5 3.9 %pad.8.occ_hbm = bf16[3072,512]{1,0:T(8,128)(2,1)} pad(bf16[3000,500]{1,0:T(8,128)(2,1)} %param.6, bf16[]{:T(256)} %constant.1.clone.1), padding=0_72x0_12 | pad | bytes 6145730 | tf_op jit(solution)/shard_map/jit(_pad)/pad | solution.py:417
  9.4 208.9 %gather.1 = (bf16[2,3072,512]{2,1,0:T(8,128)(2,1)}, bf16[4,128,3000]{2,1,0:T(8,128)(2,1)}) custom-call(bf16[2,3000,3000]{2,1,0:T(8,128)(2,1)} %h_hbm.1, bf16[3072,512]{1,0:T(8,128)(2,1)} %pad.8.occ_hbm, bf16[128,3000]{1,0:T(8,128)(2,1)} %bitcast.8, f32[4,2,1,256]{3,2,1,0:T(1,128)} %reshape.11.occ_e, f32[1024,1]{1,0:T(8,128)} %bitcast.9), custom_call_target="tpu_custom_call" | custom-call | tf_op jit(solution)/shard_map/gather/pallas_call | solution.py:426
  218.3 26.0 %final.1 = bf16[2,3000,3000]{2,1,0:T(8,128)(2,1)} custom-call(bf16[2,3072,512]{2,1,0:T(8,128)(2,1)} %get-tuple-element.7.mixed_ref, bf16[512,3000]{1,0:T(8,128)(2,1)} %bitcast.7), custom_call_target="tpu_custom_call" | custom-call | tf_op jit(solution)/shard_map/final/pallas_call | solution.py:460
  (2 shorter events, 0.0 us)

commit v2 on v1

--- a/solution.py
+++ b/solution.py
@@ -13,6 +13,7 @@
 NT = (((1,), (1,)), ((), ()))
 NN = (((1,), (0,)), ((), ()))
 PIECES = 4
+HELD = 0
 
 
 def up(value, step):
@@ -42,13 +43,13 @@
     dims,
     h_hbm, occ_hbm, vir_hbm, occ_e, vir_e,
     mixed_hbm, virt_hbm,
-    occ, virt, hbuf, image, part, rs1, rs2s, rs2r, resp, acc, stage,
+    occ, virt, hbuf, image, part, rs1, rs2s, rs2r, resp, acc, stage, vraw,
     loc_sem, h_sem, vs_sem, vr_sem, zs_sem, zr_sem, ys_sem, yr_sem,
     a_s, a_r, b_s, b_r, c_s, c_r, d_s, d_r, o_sem,
 ):
     rows, cols = dims["rows"], dims["cols"]
     pert, ni, hb, nb = dims["pert"], dims["ni"], dims["hb"], dims["nb"]
-    nv, ip, piece, wh = dims["nv"], dims["ip"], dims["piece"], dims["wh"]
+    nv, ip, piece, wh, nr = dims["nv"], dims["ip"], dims["piece"], dims["wh"], dims["nr"]
     pv = pert * nv
     pr = pv // rows
     ps = pr // cols
@@ -64,11 +65,22 @@
 
     def half_copy(half, sem):
         return pltpu.make_async_copy(
-            occ_hbm.at[:, pl.ds(pl.multiple_of(half * wh, wh), wh)], occ.at[col, half], loc_sem.at[sem]
-        )
+            occ_hbm.at[:, pl.ds(pl.multiple_of(half * wh, wh), wh)], occ.at[col, half, pl.ds(0, nr)], loc_sem.at[sem]
+        )
+
+    def rows_of(q):
+        return pl.ds(q * piece, min(piece, nr - q * piece))
+
+    def whole(block, half):
+        return occ.at[block, half, pl.ds(0, nr)]
+
+    if nr < ip:
+        for block in range(cols):
+            for half in range(2):
+                occ[block, half, nr:ip] = jnp.zeros((ip - nr, wh), BF16)
 
     half_copy(grp, 0).start()
-    vir_copy = pltpu.make_async_copy(vir_hbm, virt.at[row], loc_sem.at[2])
+    vir_copy = pltpu.make_async_copy(vir_hbm, vraw, loc_sem.at[2])
     vir_copy.start()
     half_copy(other, 1).start()
 
@@ -99,19 +111,17 @@
             device_id={"row": target}, device_id_type=MESH,
         )
 
-    vir_copy.wait()
     top = rows // 2
-    vir_send(row, flip(row, top), 0).start()
 
     def z_send(block, q, target, way):
-        ref = occ.at[block, grp, pl.ds(q * piece, piece)]
+        ref = occ.at[block, grp, rows_of(q)]
         return pltpu.make_async_remote_copy(
             src_ref=ref, dst_ref=ref, send_sem=zs_sem.at[way, block], recv_sem=zr_sem.at[block, q],
             device_id={"col": target}, device_id_type=MESH,
         )
 
     def y_send(block, q):
-        ref = occ.at[block, grp, pl.ds(q * piece, piece)]
+        ref = occ.at[block, grp, rows_of(q)]
         return pltpu.make_async_remote_copy(
             src_ref=ref, dst_ref=ref, send_sem=ys_sem.at[block], recv_sem=yr_sem.at[block],
             device_id={"grp": other}, device_id_type=MESH,
@@ -122,21 +132,39 @@
         pl.when(col >= 1)(lambda q=q: z_send(col, q, col - 1, 0).start())
         pl.when(col <= cols - 2)(lambda q=q: z_send(col, q, col + 1, 1).start())
 
+    vir_copy.wait()
+    size = virt.shape[1]
+    unit = lax.broadcasted_iota(jnp.int32, (size, size), 0) == lax.broadcasted_iota(jnp.int32, (size, size), 1)
+    turned = lax.dot_general(unit.astype(F32).astype(BF16), vraw[...], NT, preferred_element_type=F32)
+    virt[row] = turned.astype(BF16)
+    vir_send(row, flip(row, top), 0).start()
+
+    def forward(slot, q):
+        def to_right():
+            z_send(col - 1 - slot, q, col + 1, 1).start()
+
+        def to_left():
+            z_send(col + 1 + slot, q, col - 1, 0).start()
+
+        pl.when((col - 1 - slot >= 0) & (col <= cols - 2))(to_right)
+        pl.when((col + 1 + slot <= cols - 1) & (col >= 1))(to_left)
+
     def pump(slot, q):
         def from_left():
             block = col - 1 - slot
             z_send(block, q, 0, 1).wait_recv()
-            pl.when(col <= cols - 2)(lambda: z_send(block, q, col + 1, 1).start())
             y_send(block, q).start()
 
         def from_right():
             block = col + 1 + slot
             z_send(block, q, 0, 0).wait_recv()
-            pl.when(col >= 1)(lambda: z_send(block, q, col - 1, 0).start())
             y_send(block, q).start()
 
         pl.when(col - 1 - slot >= 0)(from_left)
         pl.when(col + 1 + slot <= cols - 1)(from_right)
+        before = slot * PIECES + q - HELD
+        if before >= 0 and before // PIECES <= cols - 3:
+            forward(before // PIECES, before % PIECES)
 
     pump(0, 0)
     held, bit = [0], top
@@ -196,7 +224,7 @@
         block, second, half = chunk(s)
         if s >= 2:
             def await_second():
-                pltpu.make_async_copy(occ.at[block, half], occ.at[block, half], yr_sem.at[block]).wait()
+                pltpu.make_async_copy(whole(block, half), whole(block, half), yr_sem.at[block]).wait()
             pl.when(second == 1)(await_second)
 
         def body(d, carry):
@@ -238,11 +266,11 @@
             device_id={"col": (col + e) % cols}, device_id_type=MESH,
         )
 
-    def ag2_send(block, half, d):
-        ref = resp.at[block, half, row]
-        return pltpu.make_async_remote_copy(
-            src_ref=ref, dst_ref=ref, send_sem=d_s.at[block, half], recv_sem=d_r.at[block, half],
-            device_id={"row": (row + d) % rows}, device_id_type=MESH,
+    def ag2_send(block, half, owner, target, n):
+        ref = resp.at[block, half, owner]
+        return pltpu.make_async_remote_copy(
+            src_ref=ref, dst_ref=ref, send_sem=d_s.at[block, half], recv_sem=d_r.at[block, half, n],
+            device_id={"row": target}, device_id_type=MESH,
         )
 
     def respond(d, second):
@@ -251,7 +279,10 @@
             total = rs2s[block, half, col].astype(F32)
             for e in range(cols - 1):
                 total = total + rs2r[block, half, e].astype(F32)
-            gaps = occ_e[block, half] - vir_e[pl.ds(pl.multiple_of(row * pr + col * ps, ps), ps), :]
+            state = (row * pr + col * ps) % nv + lax.broadcasted_iota(jnp.int32, (ps, nv), 0)
+            lane = lax.broadcasted_iota(jnp.int32, (ps, nv), 1)
+            levels = jnp.sum(jnp.where(lane == state, vir_e[...], 0.0), axis=1, keepdims=True)
+            gaps = occ_e[block, half] - levels
             resp[block, half, row, col] = (total / gaps).astype(BF16)
             for e in range(1, cols):
                 ag1_send(block, half, e).start()
@@ -260,8 +291,26 @@
         for block, half in pair(d, second):
             some = resp.at[block, half, row, pl.ds(0, cols - 1)]
             pltpu.make_async_copy(some, some, c_r.at[block, half]).wait()
-            for e in range(1, rows):
-                ag2_send(block, half, e).start()
+            ag2_send(block, half, row, flip(row, top), 0).start()
+            if top > 1:
+                ag2_send(block, half, row, flip(row, 1), rows - 2).start()
+
+    def relay(d, second):
+        held, bit, base = [0], top, 0
+        while bit >= 1:
+            for block, half in pair(d, second):
+                for n, h in enumerate(held):
+                    early = h == 0 and (bit == top or bit == 1)
+                    if not early:
+                        place = base + n if bit > 1 or n > 0 else rows - 2
+                        place = base + n - 1 if bit == 1 and top > 1 else place
+                        ag2_send(block, half, flip_all(row, h), flip(row, bit), place).start()
+            for block, half in pair(d, second):
+                for n in range(len(held)):
+                    ag2_send(block, half, row, row, base + n).wait_recv()
+            base += len(held)
+            held = held + [h + bit for h in held]
+            bit //= 2
 
     tile = dims["tile"]
     tiles = ip // tile
@@ -276,9 +325,6 @@
 
     def mix(d, second, first, last):
         chunks = pair(d, second)
-        for block, half in chunks:
-            some = resp.at[block, half, pl.ds(0, rows - 1)]
-            pltpu.make_async_copy(some, some, d_r.at[block, half]).wait()
 
         def body(n, carry):
             at = pl.ds(pl.multiple_of(n * tile, tile), tile)
@@ -334,40 +380,54 @@
     some_pumps(1, 1)
     combine(3)
     through(1)
-    started = False
-    for s in range(4, cols + 1):
+    for s in range(4, cols):
         through((s - 2) // 2)
         make_part(s)
         some_pumps(1, (s - 2) // 2 + 1)
         combine(s)
-    for d in range(cols // 2):
-        s = cols + 2 * d
-        if d > 0:
-            through((s - 2) // 2)
-            make_part(s)
-            combine(s)
-        final = d == cols // 2 - 1
+    through((cols - 2) // 2)
+    make_part(cols)
+    combine(cols)
+    some_pumps(1, cols // 2)
+    make_part(cols + 1)
+    respond(0, 0)
+    some_pumps(1, cols // 2)
+    combine(cols + 1)
+    spread(0, 0)
+    some_pumps(1, cols // 2)
+    respond(0, 1)
+    pairs = cols // 2
+    for d in range(pairs - 1):
+        s = cols + 2 * d + 2
+        through((s - 2) // 2)
+        make_part(s)
+        relay(d, 0)
+        spread(d, 1)
+        some_pumps(1, s // 2)
+        combine(s)
+        mix(d, 0, d == 0, False)
+        some_pumps(1, s // 2)
+        relay(d, 1)
         make_part(s + 1)
-        respond(d, 0)
+        respond(d + 1, 0)
         some_pumps(1, s // 2)
+        mix(d, 1, False, False)
         combine(s + 1)
-        spread(d, 0)
+        spread(d + 1, 0)
         some_pumps(1, s // 2)
-        respond(d, 1)
-        mix(d, 0, not started, False)
-        started = True
-        some_pumps(1, s // 2)
-        spread(d, 1)
-        mix(d, 1, False, final)
+        respond(d + 1, 1)
+    relay(pairs - 1, 0)
+    spread(pairs - 1, 1)
+    mix(pairs - 1, 0, pairs == 1, False)
+    relay(pairs - 1, 1)
+    mix(pairs - 1, 1, False, True)
 
     virt_out.wait()
     for n in range(rows - 1):
         vir_send(row, row, n).wait_send()
     for block in range(cols):
-        whole = occ.at[block, 0]
-
-        def sent(sem, whole=whole):
-            pltpu.make_async_copy(whole, whole, sem).wait()
+        def sent(sem, ref=whole(block, 0)):
+            pltpu.make_async_copy(ref, ref, sem).wait()
 
         pl.when((col >= 1) & (col <= block))(lambda: sent(zs_sem.at[0, block]))
         pl.when((col <= cols - 2) & (col >= block))(lambda: sent(zs_sem.at[1, block]))
@@ -412,13 +472,12 @@
     pr = pv // rows
     ps = pr // cols
     tile = 512 if ip % 512 == 0 else 256
-    dims = dict(rows=rows, cols=cols, pert=pert, ni=ni, hb=hb, nb=nb, nv=nv, ip=ip, piece=piece, wh=wh, tile=tile)
-
-    occ_padded = jnp.pad(occ_coeffs, ((0, ip - ni), (0, 2 * wh - width)))
-    vir_t = vir_coeffs.T
+    dims = dict(rows=rows, cols=cols, pert=pert, ni=ni, hb=hb, nb=nb, nv=nv, ip=ip, piece=piece, wh=wh, tile=tile, nr=up(ni, 16))
+
+    occ_padded = jnp.pad(occ_coeffs, ((0, up(ni, 16) - ni), (0, 2 * wh - width)))
     occ_e = jnp.pad(occ_energies.reshape(cols, width), ((0, 0), (0, 2 * wh - width)), constant_values=-1.0)
     occ_e = occ_e.reshape(cols, 2, 1, wh)
-    vir_e = jnp.tile(vir_energies, pert)[:, None]
+    vir_e = vir_energies[None, :]
 
     any_space = pl.BlockSpec(memory_space=pl.ANY)
     vmem = pl.BlockSpec(memory_space=pltpu.VMEM)
@@ -443,20 +502,21 @@
             pltpu.VMEM((cols, 2, rows, cols, ps, wh), BF16),
             pltpu.VMEM((pert, ip, nv), F32),
             pltpu.VMEM((2, pert, tile, nv), BF16),
+            pltpu.VMEM((nj, nv // rows), BF16),
             dma((3,)), dma((2,)), dma((rows,)), dma((rows,)),
             dma((2, cols)), dma((cols, PIECES)), dma((cols,)), dma((cols,)),
             dma((cols, 2)), dma((cols, 2)), dma((cols, 2)), dma((cols, 2)),
-            dma((cols, 2)), dma((cols, 2)), dma((cols, 2)), dma((cols, 2)),
+            dma((cols, 2)), dma((cols, 2)), dma((cols, 2)), dma((cols, 2, rows - 1)),
             dma((2,)),
         ],
         compiler_params=pltpu.CompilerParams(
             collective_id=0, has_side_effects=True, vmem_limit_bytes=67043328
         ),
         name="gather",
-    )(perturbation, occ_padded, vir_t, occ_e, vir_e)
+    )(perturbation, occ_padded, vir_coeffs, occ_e, vir_e)
 
     virt = virt.reshape(nv, nj)
-    block = 384 if ip % 384 == 0 else 256
+    block = 768 if ip % 768 == 0 else 256
     return pl.pallas_call(
         final_kernel,
         out_shape=jax.ShapeDtypeStruct((pert, ni, nj), BF16),

time: 246 us -> 205 us (0.83)
  Pallas kernels: 235 us -> 199 us
  local copies, waits for them, and re-layouts: 9.41 us -> 5.3 us
    pallas_call x1, Pallas kernels: 209 us -> 174 us  [per_device(): pl.pallas_call(functools.partial(gather_kernel, dims), out_shape=(jax.Sha...]
    unnamed x4 -> x0, local copies, waits for them, and re-layouts: 4.08 us -> none
where the time goes in v2:
time: 205 us; the launch traced here: 204 us
  Pallas kernels  199 us (97%)
  local copies, waits for them, and re-layouts  5.3 us (3%)
    pallas_call x1, Pallas kernels, per_device(): pl.pallas_call(functools.partial(gather_kernel, dims), out_shape=(jax.Sha...  174 us
    pallas_call x1, Pallas kernels, per_device(): pl.pallas_call(final_kernel, out_shape=jax.ShapeDtypeStruct((pert, ni, nj...  25.3 us

profile of v2, /device:TPU:0, one launch (start us, length us, event | category | flops | bytes accessed | tf_op | source)
XLA Modules:
  0.0 204.4 jit_solution(12324411075423815176)
XLA Ops:
  0.0 0.8 reshape.9
  0.8 0.6 reshape.10.occ_e
  1.4 3.9 %pad.8.occ_hbm = bf16[3008,512]{1,0:T(8,128)(2,1)} pad(bf16[3000,500]{1,0:T(8,128)(2,1)} %param.6, bf16[]{:T(256)} %constant.1.clone.1), padding=0_8x0_12 | pad | bytes 6080194 | tf_op jit(solution)/shard_map/jit(_pad)/pad | solution.py:477
  5.3 173.8 %gather.1 = (bf16[2,3072,512]{2,1,0:T(8,128)(2,1)}, bf16[4,128,3000]{2,1,0:T(8,128)(2,1)}) custom-call(bf16[2,3000,3000]{2,1,0:T(8,128)(2,1)} %h_hbm.1, bf16[3008,512]{1,0:T(8,128)(2,1)} %pad.8.occ_hbm, bf16[3000,128]{1,0:T(8,128)(2,1)} %vir_hbm.1, f32[4,2,1,256]{3,2,1,0:T(1,128)} %reshape.10.occ_e, f32[1,512]{1,0:T(1,128)} %bitcast.3), custom_call_target="tpu_custom_call" | custom-call | tf_op jit(solution)/shard_map/gather/pallas_call | solution.py:485
  179.1 25.3 %final.1 = bf16[2,3000,3000]{2,1,0:T(8,128)(2,1)} custom-call(bf16[2,3072,512]{2,1,0:T(8,128)(2,1)} %get-tuple-element.7.mixed_ref, bf16[512,3000]{1,0:T(8,128)(2,1)} %bitcast.2), custom_call_target="tpu_custom_call" | custom-call | tf_op jit(solution)/shard_map/final/pallas_call | solution.py:520
  (1 shorter events, 0.0 us)
